TPU v7x, 128 devices: a whole 4x4x4 slice. The times are simulated.
128 devices in a mesh: row: 8 (over x, z_hi), col: 4 (over z_lo, core), depth: 4 (over y).
Axes of the slice: x: 4, y: 4, z: 4 (z_hi: 2, z_lo: 2; z = z_hi * 2 + z_lo), core: 2. Of those that a mesh axis runs over, the one named last changes fastest.
Arguments:
- acts: bfloat16 [8192, 5120], P(('depth', 'col'), 'row'), may hold values from -6 to 6
- grad_out: bfloat16 [8192, 13824], P(('depth', 'row'), 'col'), may hold values from -6 to 6
- weight: bfloat16 [5120, 13824], P('row', 'col'), may hold values from -0.078125 to 0.078125
- master: float32 [5120, 13824], P(('row', 'depth'), 'col'), may hold values from -0.078125 to 0.078125
- moment_one: float32 [5120, 13824], P(('row', 'depth'), 'col'), may hold values from -4 to 4
- moment_two: float32 [5120, 13824], P(('row', 'depth'), 'col'), may hold values from 0.05 to 2
Outputs:
- grad_in: bfloat16 [8192, 5120], P(('depth', 'col'), 'row')
- new_weight: bfloat16 [5120, 13824], P('row', 'col')
- new_master: float32 [5120, 13824], P(('row', 'depth'), 'col')
- new_moment_one: float32 [5120, 13824], P(('row', 'depth'), 'col')
- new_moment_two: float32 [5120, 13824], P(('row', 'depth'), 'col')
All inputs are finite; a program needn't handle non-finite values.
Results may differ from a plain program's by a relative error of at most 0.0035.
Values may be sent and summed in bfloat16 or wider, within the bound.
A program may use at most 128 MiB of HBM per device.

v0:
```python
import math
import jax
import jax.numpy as jnp
from jax import lax
from jax.sharding import PartitionSpec as P

STEP = 10


def in_order(parts, dim):
    dims = list(parts.shape[1:])
    dims[dim] *= parts.shape[0]
    return jnp.moveaxis(parts, 0, dim).reshape(dims)


def from_everyone(array, axis):
    count = lax.axis_size(axis)
    return lax.all_to_all(
        jnp.broadcast_to(array[None], (count, *array.shape)), axis, 0, 0, tiled=True
    )


def gathered_copies(array, axis, dim):
    return in_order(from_everyone(array, axis), dim)


def cut_along(array, dim, count):
    before, after = (array.shape[:dim], array.shape[dim + 1 :])
    return jnp.moveaxis(array.reshape(*before, count, -1, *after), dim, 0)


def sum_at_owner(array, axis, dim):
    parts = cut_along(array, dim, lax.axis_size(axis))
    arrived = lax.all_to_all(parts, axis, split_axis=0, concat_axis=0, tiled=True)
    return arrived.sum(axis=0)


def per_device(acts, grad_out, weight, master, moment_one, moment_two):
    whole_acts = gathered_copies(acts, "col", 0)
    tokens_total = acts.shape[0] * lax.axis_size("col") * lax.axis_size("depth")
    whole_cotangent = lax.all_gather(grad_out, "row", axis=0, tiled=True)
    picked = whole_cotangent
    input_sum = sum_at_owner(
        lax.dot_general(
            picked, weight, (((1,), (1,)), ((), ())), preferred_element_type=jnp.float32
        ),
        "col",
        0,
    )
    picked = whole_acts
    grad_sum = lax.psum_scatter(
        lax.dot_general(
            picked, whole_cotangent, (((0,), (0,)), ((), ())), preferred_element_type=jnp.float32
        ).astype(jnp.bfloat16),
        "depth",
        scatter_dimension=0,
        tiled=True,
    ).astype(jnp.float32)
    grad_in = input_sum.astype(jnp.bfloat16)
    grad = grad_sum * jnp.float32(1.0 / math.sqrt(tokens_total))
    new_moment_one = 0.9 * moment_one + 0.1 * grad
    new_moment_two = 0.95 * moment_two + 0.05 * grad * grad
    first_fix = 1.0 - 0.9**STEP
    second_fix = 1.0 - 0.95**STEP
    update = new_moment_one / first_fix / (jnp.sqrt(new_moment_two / second_fix) + 1e-08)
    new_master = master - 0.01 * (update + 0.1 * master)
    new_weight = lax.all_gather(new_master.astype(jnp.bfloat16), "depth", axis=0, tiled=True)
    return (grad_in, new_weight, new_master, new_moment_one, new_moment_two)


def solution(mesh):
    placed = (
        P(("depth", "col"), "row"),
        P(("depth", "row"), "col"),
        P("row", "col"),
        P(("row", "depth"), "col"),
        P(("row", "depth"), "col"),
        P(("row", "depth"), "col"),
    )
    return jax.shard_map(
        per_device,
        mesh=mesh,
        in_specs=placed,
        out_specs=(
            P(("depth", "col"), "row"),
            P("row", "col"),
            P(("row", "depth"), "col"),
            P(("row", "depth"), "col"),
            P(("row", "depth"), "col"),
        ),
        check_vma=False,
    )
```

profile of v0, /device:TPU:1, one launch (start us, length us, event | category | flops | bytes accessed | tf_op | source)
XLA Modules:
  0.0 352.9 jit_solution(4790569811612537850)
XLA Ops:
  7.2 0.0 copy-start.1
  7.2 0.0 all-gather.3.cloned.1.call-start
  7.2 0.7 all-gather.3.cloned.1.call-update
  7.9 0.0 reduce-scatter.2.cloned.1.call-start
  8.0 0.3 copy-done.1
  8.3 0.2 broadcast_in_dim.2
  8.5 50.5 %all_to_all.10 = bf16[4,512,640]{2,1,0:T(8,128)(2,1)S(1)} all-to-all(bf16[4,512,640]{2,1,0:T(8,128)(2,1)S(1)} %broadcast_in_dim.2), channel_id=1, replica_groups=mesh['row'=8,'col'=4,'depth'=4] {'col'}, dimensions={0} | all-to-all | bytes 5242880 | tf_op jit(solution)/shard_map/all_to_all | solution.py:18
  59.0 131.6 %all-gather.3.cloned.1.call-done = bf16[2048,3456]{1,0:T(8,128)(2,1)} async-done(((bf16[256,3456]{1,0:T(8,128)(2,1)}), bf16[2048,3456]{1,0:T(8,128)(2,1)}) %all-gather.3.cloned.1.call-update) | async-done | bytes 14155792 | tf_op jit(solution)/shard_map/all_gather | solution.py:41
  190.6 14.4 %convolution_convert_fusion = bf16[640,3456]{1,0:T(8,128)(2,1)} fusion(bf16[2048,640]{1,0:T(8,128)(2,1)S(1)} %bitcast.7, bf16[2048,3456]{1,0:T(8,128)(2,1)} %all-gather.3.cloned.1.call-done), kind=kOutput, calls=%fused_computation | convolution fusion | flops 9061908480 | bytes 21200896 | tf_op jit(solution)/shard_map/dot_general | solution.py:52
  205.1 0.0 copy-start
  205.1 0.0 reduce-scatter.2.cloned.1.call-update
  205.1 0.0 all-gather.5.cloned.1.call-start
  205.1 47.2 %reduce-scatter.2.cloned.1.call-done = bf16[160,3456]{1,0:T(8,128)(2,1)} async-done(((bf16[640,3456]{1,0:T(8,128)(2,1)}), bf16[160,3456]{1,0:T(8,128)(2,1)}) %reduce-scatter.2.cloned.1.call-update) | async-done | bytes 1105936 | tf_op jit(solution)/shard_map/reduce_scatter | solution.py:51
  252.3 0.0 copy-done
  252.3 7.0 %fusion.3 = (bf16[160,3456]{1,0:T(8,128)(2,1)}, f32[160,3456]{1,0:T(8,128)}, f32[160,3456]{1,0:T(8,128)}, f32[160,3456]{1,0:T(8,128)}) fusion(f32[160,3456]{1,0:T(8,128)S(1)} %copy-done, bf16[160,3456]{1,0:T(8,128)(2,1)} %reduce-scatter.2.cloned.1.call-done, f32[160,3456]{1,0:T(8,128)} %param.10, f32[160,3456]{1,0:T(8,128)} %param.11), kind=kLoop, calls=%fused_computation.8 | loop fusion | flops 9953280 | bytes 15482880 | tf_op jit(solution)/shard_map/convert_element_type | solution.py:67
  259.4 0.0 all-gather.5.cloned.1.call-update
  259.4 15.9 %fusion.6 = f32[2048,640]{1,0:T(8,128)S(1)} fusion(bf16[2048,3456]{1,0:T(8,128)(2,1)} %all-gather.3.cloned.1.call-done, bf16[640,3456]{1,0:T(8,128)(2,1)} %param.8), kind=kOutput, calls=%fused_computation.9 | convolution fusion | flops 9059696640 | bytes 23822336 | tf_op jit(solution)/shard_map/dot_general | solution.py:44
  275.3 62.6 %all_to_all.11 = f32[4,512,640]{2,1,0:T(8,128)} all-to-all(f32[4,512,640]{2,1,0:T(8,128)S(1)} %bitcast.6), channel_id=1, replica_groups=mesh['row'=8,'col'=4,'depth'=4] {'col'}, dimensions={0} | all-to-all | bytes 10485760 | tf_op jit(solution)/shard_map/all_to_all | solution.py:34
  337.9 3.8 %reduce_sum.9 = bf16[512,640]{1,0:T(8,128)(2,1)} reduce(f32[4,512,640]{2,1,0:T(8,128)} %all_to_all.11, f32[]{:T(128)} %constant.4.clone.1), dimensions={0}, to_apply=%region_0.0 | reduce | flops 983040 | bytes 5898244 | tf_op jit(solution)/shard_map/reduce_sum | solution.py:35
  341.7 0.0 all-gather.5.cloned.1.call-done
  341.7 4.6 %copy.12 = bf16[640,3456]{1,0:T(8,128)(2,1)} copy(bf16[640,3456]{1,0:T(8,128)(2,1)} %all-gather.5.cloned.1.call-done) | data formatting | bytes 8847360
Async XLA Ops:
  7.2 1.1 copy-start.1
  7.2 183.5 %all-gather.3.cloned.1.call-start = ((), (), s32[]{:S(2)}) async-start(), calls=%async_computation.3 | async-start | bytes 15925248 | tf_op jit(solution)/shard_map/all_gather | solution.py:41
  7.9 244.4 %reduce-scatter.2.cloned.1.call-start = ((), (), s32[]{:S(2)}) async-start(), calls=%async_computation.4 | async-start | bytes 5529600 | tf_op jit(solution)/shard_map/reduce_scatter | solution.py:51
  205.1 47.3 %copy-start = (f32[160,3456]{1,0:T(8,128)S(1)}, f32[160,3456]{1,0:T(8,128)}, u32[]{:S(2)}) copy-start(f32[160,3456]{1,0:T(8,128)} %param.9) | copy-start | bytes 6635524
  205.1 136.6 %all-gather.5.cloned.1.call-start = ((), (), s32[]{:S(2)}) async-start(), calls=%async_computation.5 | async-start | bytes 5529600 | tf_op jit(solution)/shard_map/all_gather | solution.py:67
Sparse Core Ops, SparseCore 0:
  10.3 180.2 all-gather.2
  205.2 47.0 reduce-scatter.1
  259.5 49.7 all-gather.4
where the time goes:
time: 353 us
  waiting for transfers between devices  180 us (51%)
  blocking collectives  113 us (32%)
  matrix products  30.3 us (9%)
  between operations  13.8 us (4%)
  other arithmetic  10.8 us (3%)
  local copies, waits for them, and re-layouts  5.15 us (1%)
    all_gather x1, waiting for transfers between devices, per_device(): whole_cotangent = lax.all_gather(grad_out, 'row', axis=0, tiled=True)  132 us
    all_to_all x1, blocking collectives, sum_at_owner(): lax.all_to_all(parts, axis, split_axis=0, concat_axis=0, tiled=True)  62.6 us
    all_to_all x1, blocking collectives, from_everyone(): lax.all_to_all(jnp.broadcast_to(array[None], (count, *array.shape)), axis...  50.5 us
    reduce_scatter x1, waiting for transfers between devices, per_device(): lax.psum_scatter(lax.dot_general(picked, whole_cotangent, (((0,), (0,)),...  47.2 us
    dot_general x1, matrix products, per_device(): lax.dot_general(picked, weight, (((1,), (1,)), ((), ())), preferred_eleme...  15.9 us
    dot_general x1, matrix products, per_device(): lax.dot_general(picked, whole_cotangent, (((0,), (0,)), ((), ())), prefer...  14.4 us
  transfers between devices with their start and end apart: 3, of which 2 were waited for; matrix products, arithmetic and copies ran while one was open for 6% of the time, Pallas kernels for 0%

commit v1 on v0

--- a/solution.py
+++ b/solution.py
@@ -38,7 +38,9 @@
 def per_device(acts, grad_out, weight, master, moment_one, moment_two):
     whole_acts = gathered_copies(acts, "col", 0)
     tokens_total = acts.shape[0] * lax.axis_size("col") * lax.axis_size("depth")
-    whole_cotangent = lax.all_gather(grad_out, "row", axis=0, tiled=True)
+    whole_cotangent = jnp.concatenate(
+        lax.all_to_all(jnp.stack([grad_out] * lax.axis_size("row")), "row", 0, 0), axis=0
+    )
     picked = whole_cotangent
     input_sum = sum_at_owner(
         lax.dot_general(

time: 353 us -> 375 us (1.062)
  blocking collectives: 113 us -> 260 us
  waiting for transfers between devices: 180 us -> 49.9 us
  local copies, waits for them, and re-layouts: 5.15 us -> 12.3 us
    all_to_all x0 -> x1, blocking collectives: none -> 163 us  [per_device(): lax.all_to_all(jnp.stack([grad_out] * lax.axis_size('row')), 'row', 0, 0)]
    all_gather x1 -> x0, waiting for transfers between devices: 132 us -> none  [per_device(): whole_cotangent = lax.all_gather(grad_out, 'row', axis=0, tiled=True)]
    all_to_all x1, blocking collectives: 50.5 us -> 34.9 us  [from_everyone(): lax.all_to_all(jnp.broadcast_to(array[None], (count, *array.shape)), axis...]
    unnamed x5 -> x7, local copies, waits for them, and re-layouts: 4.95 us -> 9.72 us
  transfers between devices with their start and end apart: 3 -> 2, of which waited for: 2 -> 1; matrix products, arithmetic and copies ran while one was open for 6% -> 5% of each run, Pallas kernels for 0% -> 0%
where the time goes in v1:
time: 375 us
  blocking collectives  260 us (69%)
  waiting for transfers between devices  49.9 us (13%)
  matrix products  27.5 us (7%)
  between operations  14.1 us (4%)
  local copies, waits for them, and re-layouts  12.3 us (3%)
  other arithmetic  10.8 us (3%)
    all_to_all x1, blocking collectives, per_device(): lax.all_to_all(jnp.stack([grad_out] * lax.axis_size('row')), 'row', 0, 0)  163 us
    all_to_all x1, blocking collectives, sum_at_owner(): lax.all_to_all(parts, axis, split_axis=0, concat_axis=0, tiled=True)  62.6 us
    reduce_scatter x1, waiting for transfers between devices, per_device(): lax.psum_scatter(lax.dot_general(picked, whole_cotangent, (((0,), (0,)),...  49.9 us
    all_to_all x1, blocking collectives, from_everyone(): lax.all_to_all(jnp.broadcast_to(array[None], (count, *array.shape)), axis...  34.9 us
    dot_general x1, matrix products, per_device(): lax.dot_general(picked, weight, (((1,), (1,)), ((), ())), preferred_eleme...  15.9 us
    dot_general x1, matrix products, per_device(): lax.dot_general(picked, whole_cotangent, (((0,), (0,)), ((), ())), prefer...  11.5 us
    unnamed x7, local copies, waits for them, and re-layouts  9.72 us
  transfers between devices with their start and end apart: 2, of which 1 were waited for; matrix products, arithmetic and copies ran while one was open for 5% of the time, Pallas kernels for 0%

profile of v1, /device:TPU:1, one launch (start us, length us, event | category | flops | bytes accessed | tf_op | source)
XLA Modules:
  0.0 374.7 jit_solution(14685978226077649701)
XLA Ops:
  7.2 0.0 reduce-scatter.2.cloned.1.call-start
  7.2 1.3 broadcast_in_dim.2
  8.5 0.0 copy-start.2
  8.5 34.9 %all_to_all.15 = bf16[4,512,640]{2,1,0:T(8,128)(2,1)S(1)} all-to-all(bf16[4,512,640]{2,1,0:T(8,128)(2,1)S(1)} %broadcast_in_dim.2), channel_id=1, replica_groups=mesh['row'=8,'col'=4,'depth'=4] {'col'}, dimensions={0} | all-to-all | bytes 5242880 | tf_op jit(solution)/shard_map/all_to_all | solution.py:18
  43.4 0.0 copy-done.2
  43.4 1.3 stack.2
  44.7 162.6 %all_to_all.16 = bf16[8,256,3456]{2,1,0:T(8,128)(2,1)S(1)} all-to-all(bf16[8,256,3456]{2,1,0:T(8,128)(2,1)S(1)} %stack.2), channel_id=1, replica_groups=mesh['row'=8,'col'=4,'depth'=4] {'row'}, dimensions={0} | all-to-all | bytes 28311552 | tf_op jit(solution)/shard_map/all_to_all | solution.py:42
  207.3 0.0 copy-start
  207.3 5.1 %copy-done = bf16[8,256,3456]{2,1,0:T(8,128)(2,1)} copy-done((bf16[8,256,3456]{2,1,0:T(8,128)(2,1)}, bf16[8,256,3456]{2,1,0:T(8,128)(2,1)S(1)}, u32[]{:S(2)}) %copy-start) | copy-done | bytes 14155800
  212.4 11.5 %convolution_convert_fusion = bf16[640,3456]{1,0:T(8,128)(2,1)} fusion(bf16[2048,640]{1,0:T(8,128)(2,1)S(1)} %bitcast.11, bf16[2048,3456]{1,0:T(8,128)(2,1)S(1)} %bitcast.9), kind=kOutput, calls=%fused_computation | convolution fusion | flops 9061908480 | bytes 21200896 | tf_op jit(solution)/shard_map/dot_general | solution.py:54
  223.9 0.0 copy-start.1
  223.9 0.0 reduce-scatter.2.cloned.1.call-update
  223.9 0.0 all-gather.2.cloned.1.call-start
  224.0 49.9 %reduce-scatter.2.cloned.1.call-done = bf16[160,3456]{1,0:T(8,128)(2,1)} async-done(((bf16[640,3456]{1,0:T(8,128)(2,1)}), bf16[160,3456]{1,0:T(8,128)(2,1)}) %reduce-scatter.2.cloned.1.call-update) | async-done | bytes 1105936 | tf_op jit(solution)/shard_map/reduce_scatter | solution.py:53
  273.8 0.0 copy-done.1
  273.8 7.0 %fusion.5 = (bf16[160,3456]{1,0:T(8,128)(2,1)}, f32[160,3456]{1,0:T(8,128)}, f32[160,3456]{1,0:T(8,128)}, f32[160,3456]{1,0:T(8,128)}) fusion(f32[160,3456]{1,0:T(8,128)S(1)} %copy-done.1, bf16[160,3456]{1,0:T(8,128)(2,1)} %reduce-scatter.2.cloned.1.call-done, f32[160,3456]{1,0:T(8,128)} %param.10, f32[160,3456]{1,0:T(8,128)} %param.11), kind=kLoop, calls=%fused_computation.10 | loop fusion | flops 9953280 | bytes 15482880 | tf_op jit(solution)/shard_map/convert_element_type | solution.py:69
  280.9 0.0 all-gather.2.cloned.1.call-update
  280.9 15.9 %fusion = f32[4,512,640]{2,1,0:T(8,128)S(1)} fusion(bf16[4,512,3456]{2,1,0:T(8,128)(2,1)} %bitcast.10, bf16[640,3456]{1,0:T(8,128)(2,1)} %param.8), kind=kOutput, calls=%fused_computation.1 | convolution fusion | flops 9059696640 | bytes 23822336 | tf_op jit(solution)/shard_map/dot_general | solution.py:46
  296.8 62.6 %all_to_all.17 = f32[4,512,640]{2,1,0:T(8,128)} all-to-all(f32[4,512,640]{2,1,0:T(8,128)S(1)} %fusion), channel_id=1, replica_groups=mesh['row'=8,'col'=4,'depth'=4] {'col'}, dimensions={0} | all-to-all | bytes 10485760 | tf_op jit(solution)/shard_map/all_to_all | solution.py:34
  359.4 3.8 %reduce_sum.9 = bf16[512,640]{1,0:T(8,128)(2,1)} reduce(f32[4,512,640]{2,1,0:T(8,128)} %all_to_all.17, f32[]{:T(128)} %constant.4.clone.1), dimensions={0}, to_apply=%region_0.0 | reduce | flops 983040 | bytes 5898244 | tf_op jit(solution)/shard_map/reduce_sum | solution.py:35
  363.2 0.0 all-gather.2.cloned.1.call-done
  363.2 4.6 %copy.12 = bf16[640,3456]{1,0:T(8,128)(2,1)} copy(bf16[640,3456]{1,0:T(8,128)(2,1)} %all-gather.2.cloned.1.call-done) | data formatting | bytes 8847360
Async XLA Ops:
  7.2 266.7 %reduce-scatter.2.cloned.1.call-start = ((), (), s32[]{:S(2)}) async-start(), calls=%async_computation.4 | async-start | bytes 5529600 | tf_op jit(solution)/shard_map/reduce_scatter | solution.py:53
  8.5 34.9 %copy-start.2 = (bf16[256,3456]{1,0:T(8,128)(2,1)S(1)}, bf16[256,3456]{1,0:T(8,128)(2,1)}, u32[]{:S(2)}) copy-start(bf16[256,3456]{1,0:T(8,128)(2,1)} %param.7) | copy-start | bytes 5308420
  207.3 5.1 %copy-start = (bf16[8,256,3456]{2,1,0:T(8,128)(2,1)}, bf16[8,256,3456]{2,1,0:T(8,128)(2,1)S(1)}, u32[]{:S(2)}) copy-start(bf16[8,256,3456]{2,1,0:T(8,128)(2,1)S(1)} %all_to_all.16) | copy-start | bytes 42467332
  223.9 50.0 %copy-start.1 = (f32[160,3456]{1,0:T(8,128)S(1)}, f32[160,3456]{1,0:T(8,128)}, u32[]{:S(2)}) copy-start(f32[160,3456]{1,0:T(8,128)} %param.9) | copy-start | bytes 6635524
  223.9 139.3 %all-gather.2.cloned.1.call-start = ((), (), s32[]{:S(2)}) async-start(), calls=%async_computation.5 | async-start | bytes 5529600 | tf_op jit(solution)/shard_map/all_gather | solution.py:69
Sparse Core Ops, SparseCore 0:
  224.0 49.7 reduce-scatter.1
  281.0 49.7 all-gather.1
